TPU v7x, 32 devices: a whole 2x2x4 slice. The times are simulated.
32 devices in a mesh: dp: 4 (over x, core), expert: 8 (over z, y).
Axes of the slice: x: 2, y: 2, z: 4, core: 2. Of those that a mesh axis runs over, the one named last changes fastest.
Arguments:
- tokens: bfloat16 [4096, 1024], P(('dp', 'expert')), may hold values from -6 to 6
- task_ids: int32 [32], P('dp'), may hold values from 0 to 5
- routing: int32 [32, 2], P('dp'), may hold values from 0 to 7, all different within a row; in each aligned block of 8 rows (0 to 7, 8 to 15, ...) at most 3 rows name the same one
- gate_weight: bfloat16 [1024, 48], replicated, may hold values from -0.1875 to 0.1875
- w_in: bfloat16 [8, 1024, 4096], P('expert', None, 'dp'), may hold values from -0.1875 to 0.1875
- w_out: bfloat16 [8, 4096, 1024], P('expert', 'dp'), may hold values from -0.09375 to 0.09375
Outputs:
- mixed: bfloat16 [4096, 1024], P(('dp', 'expert'))
Inputs may be any that keep to these rules, and one draw needn't show every extreme that they name: `routing`: each row names two different experts. Within the 8 blocks of one index of dp no expert is named more than 3 times, a bound that some block reaches.
All inputs are finite; a program needn't handle non-finite values.
Results may differ from a plain program's by a relative error of at most 0.015.
Values may be sent and summed in bfloat16 or wider, within the bound.
A program may use at most 64 MiB of HBM per device.

v0:
```python
import jax
import jax.numpy as jnp
from jax import lax
from jax.sharding import PartitionSpec as P

BLK = 128


def shards(tokens, task_ids, routing, gate_weight, w_in, w_out):
    n_experts = lax.axis_size("expert")
    my_expert = lax.axis_index("expert")
    local_rows = tokens.shape[0]
    width_model = tokens.shape[1]
    block_total = routing.shape[0]
    block_here = local_rows // BLK
    capacity = 2 * block_here + 1
    chosen = routing == my_expert
    taken_flag = jnp.any(chosen, axis=1).astype(jnp.int32)
    ranked = jnp.cumsum(taken_flag) - taken_flag
    slot_ids = jnp.arange(capacity, dtype=jnp.int32)
    select_mask = (taken_flag[None, :] == 1) & (ranked[None, :] == slot_ids[:, None])
    select_float = select_mask.astype(jnp.bfloat16)
    select_int = select_mask.astype(jnp.int32)
    other_id = jnp.where(chosen[:, 0], routing[:, 1], routing[:, 0])
    slot_task = jnp.sum(select_int * task_ids[None, :], axis=1)
    slot_other = jnp.sum(select_int * other_id[None, :], axis=1)
    slot_valid = jnp.sum(select_int, axis=1).astype(jnp.float32)
    own_routes = lax.dynamic_slice_in_dim(routing, my_expert * block_here, block_here, 0)
    target_ids = jnp.arange(n_experts, dtype=jnp.int32)
    to_target = jnp.any(own_routes[None, :, :] == target_ids[:, None, None], axis=2).astype(
        jnp.bfloat16
    )
    outgoing = (
        to_target[:, :, None, None] * tokens.reshape(block_here, BLK, width_model)[None]
    ).reshape(n_experts * local_rows, width_model)
    arrived = lax.all_to_all(outgoing, "expert", split_axis=0, concat_axis=0, tiled=True).reshape(
        block_total, BLK, width_model
    )
    picked = (
        jnp.einsum("cm,mbd->cbd", select_float, arrived, preferred_element_type=jnp.float32)
        .astype(jnp.bfloat16)
        .reshape(capacity * BLK, width_model)
    )
    gate_columns = gate_weight.shape[1]
    logits = jnp.dot(picked, gate_weight, preferred_element_type=jnp.float32).reshape(
        capacity, BLK, gate_columns
    )
    column_ids = jnp.arange(gate_columns, dtype=jnp.int32)
    onehot_self = (column_ids[None, :] == (slot_task * n_experts + my_expert)[:, None]).astype(
        jnp.float32
    )
    onehot_other = (column_ids[None, :] == (slot_task * n_experts + slot_other)[:, None]).astype(
        jnp.float32
    )
    logit_self = jnp.sum(logits * onehot_self[:, None, :], axis=2)
    logit_other = jnp.sum(logits * onehot_other[:, None, :], axis=2)
    weights = (jax.nn.sigmoid(logit_self - logit_other) * slot_valid[:, None]).reshape(
        capacity * BLK
    )
    hidden = jax.nn.gelu(
        jnp.dot(
            picked,
            lax.all_gather(w_in[0], "dp", axis=1, tiled=True),
            preferred_element_type=jnp.float32,
        )
    ).astype(jnp.bfloat16)
    slice_width = w_out.shape[1]
    running = jnp.zeros((capacity * BLK, width_model), jnp.float32)
    segment = lax.all_gather(w_out[0], "dp", axis=0, tiled=True)
    for column_shard in range(segment.shape[0] // slice_width):
        hidden_part = lax.dynamic_slice_in_dim(hidden, column_shard * slice_width, slice_width, 1)
        weight_part = segment[column_shard * slice_width : (column_shard + 1) * slice_width]
        rounded = jnp.dot(hidden_part, weight_part, preferred_element_type=jnp.float32).astype(
            jnp.bfloat16
        )
        running = running + lax.optimization_barrier(rounded).astype(jnp.float32)
    gated = (weights[:, None] * running).astype(jnp.bfloat16).reshape(capacity, BLK, width_model)
    placed = (
        jnp.einsum("cm,cbd->mbd", select_float, gated, preferred_element_type=jnp.float32)
        .astype(jnp.bfloat16)
        .reshape(block_total * BLK, width_model)
    )
    returned = lax.all_to_all(placed, "expert", split_axis=0, concat_axis=0, tiled=True).reshape(
        n_experts, local_rows, width_model
    )
    combined = jnp.sum(returned.astype(jnp.float32), axis=0)
    return combined.astype(jnp.bfloat16)


def solution(mesh):
    placed = (
        P(("dp", "expert"), None),
        P("dp"),
        P("dp", None),
        P(),
        P("expert", None, "dp"),
        P("expert", "dp", None),
    )
    return jax.shard_map(
        shards, mesh=mesh, in_specs=placed, out_specs=P(("dp", "expert"), None), check_vma=False
    )
```

profile of v0, /device:TPU:0, one launch (start us, length us, event | category | flops | bytes accessed | tf_op | source)
XLA Modules:
  0.0 204.7 jit_solution(6801272901661402154)
XLA Ops:
  6.5 0.0 copy-start
  6.5 0.0 all-gather.5.cloned.1.call-start
  6.5 0.7 all-gather.5.cloned.1.call-update
  7.3 0.0 all-gather.7.cloned.1.call-start
  7.3 0.7 all-gather.7.cloned.1.call-update
  8.0 0.0 copy-done.2
  8.0 0.2 dynamic-slice_reduce_fusion
  8.2 0.1 compare_reduce_fusion
  8.3 0.0 copy-start.3
  8.3 1.6 broadcast_multiply_fusion
  9.9 7.3 %all-to-all-start = ((bf16[8,128,1024]{2,1,0:T(8,128)(2,1)}), bf16[8,128,1024]{2,1,0:T(8,128)(2,1)S(1)}, u32[]{:S(2)}, u32[]{:S(2)}) async-start(bf16[8,128,1024]{2,1,0:T(8,128)(2,1)} %broadcast_multiply_fusion), calls=%async_computation | async-start | bytes 4194304 | tf_op jit(solution)/shard_map/all_to_all | solution.py:36
  17.2 0.2 reduce-window.8
  17.4 0.2 convert_reduce_fusion
  17.6 0.1 fusion.30
  17.7 47.8 %all-to-all-done = bf16[8,128,1024]{2,1,0:T(8,128)(2,1)S(1)} async-done(((bf16[8,128,1024]{2,1,0:T(8,128)(2,1)}), bf16[8,128,1024]{2,1,0:T(8,128)(2,1)S(1)}, u32[]{:S(2)}, u32[]{:S(2)}) %all-to-all-start) | async-done | bytes 2097184 | tf_op jit(solution)/shard_map/all_to_all | solution.py:36
  65.4 1.4 fusion.16
  66.9 0.3 copy.31
  67.2 0.4 multiply_reduce_fusion
  67.5 0.1 multiply_bitcast_fusion
  67.6 2.3 %all-gather.5.cloned.1.call-done = bf16[1,1024,4096]{2,1,0:T(8,128)(2,1)} async-done(((bf16[1,1024,1024]{2,1,0:T(8,128)(2,1)}), bf16[1,1024,4096]{2,1,0:T(8,128)(2,1)}) %all-gather.5.cloned.1.call-update) | async-done | bytes 8388624 | tf_op jit(solution)/shard_map/all_gather | solution.py:63
  69.9 9.6 %fusion.9 = bf16[384,4096]{1,0:T(8,128)(2,1)} fusion(bf16[384,1024]{1,0:T(8,128)(2,1)S(1)} %bitcast.48, bf16[1,1024,4096]{2,1,0:T(8,128)(2,1)} %all-gather.5.cloned.1.call-done), kind=kOutput, calls=%fused_computation.10 | convolution fusion | flops 3235381248 | bytes 12320768 | tf_op jit(solution)/shard_map/dot_general | solution.py:61
  79.5 50.3 %all-gather.7.cloned.1.call-done = bf16[1,4096,1024]{2,1,0:T(8,128)(2,1)} async-done(((bf16[1,1024,1024]{2,1,0:T(8,128)(2,1)}), bf16[1,4096,1024]{2,1,0:T(8,128)(2,1)}) %all-gather.7.cloned.1.call-update) | async-done | bytes 8388624 | tf_op jit(solution)/shard_map/all_gather | solution.py:69
  129.8 3.0 %fusion.18 = bf16[384,1024]{1,0:T(8,128)(2,1)S(1)} fusion(bf16[1,4096,1024]{2,1,0:T(8,128)(2,1)} %all-gather.7.cloned.1.call-done, bf16[384,4096]{1,0:T(8,128)(2,1)} %fusion.9), kind=kOutput, calls=%fused_computation.24 | convolution fusion | flops 805699584 | bytes 3670016 | tf_op jit(solution)/shard_map/dot_general | solution.py:73
  132.7 3.1 %fusion.19 = bf16[384,1024]{1,0:T(8,128)(2,1)S(1)} fusion(bf16[1,4096,1024]{2,1,0:T(8,128)(2,1)} %all-gather.7.cloned.1.call-done, bf16[384,4096]{1,0:T(8,128)(2,1)} %fusion.9), kind=kOutput, calls=%fused_computation.25 | convolution fusion | flops 805699584 | bytes 3670016 | tf_op jit(solution)/shard_map/dot_general | solution.py:73
  135.8 0.0 copy-done.4
  135.9 2.1 %fusion.20 = bf16[384,1024]{1,0:T(8,128)(2,1)S(1)} fusion(bf16[1,4096,1024]{2,1,0:T(8,128)(2,1)S(1)} %copy-done.4, bf16[384,4096]{1,0:T(8,128)(2,1)} %fusion.9), kind=kOutput, calls=%fused_computation.26 | convolution fusion | flops 805699584 | bytes 3670016 | tf_op jit(solution)/shard_map/dot_general | solution.py:73
  138.0 2.1 %fusion.21 = bf16[384,1024]{1,0:T(8,128)(2,1)S(1)} fusion(bf16[1,4096,1024]{2,1,0:T(8,128)(2,1)S(1)} %copy-done.4, bf16[384,4096]{1,0:T(8,128)(2,1)} %fusion.9), kind=kOutput, calls=%fused_computation.27 | convolution fusion | flops 805699584 | bytes 3670016 | tf_op jit(solution)/shard_map/dot_general | solution.py:73
  140.1 0.4 multiply_convert_fusion
  140.6 1.1 convolution_convert_fusion
  141.7 1.2 copy.25
  142.9 53.9 %all_to_all.12 = bf16[8,128,1024]{2,1,0:T(8,128)(2,1)S(1)} all-to-all(bf16[8,128,1024]{2,1,0:T(8,128)(2,1)S(1)} %copy.25), channel_id=1, replica_groups=mesh['dp'=4,'expert'=8] {'expert'}, dimensions={0} | all-to-all | bytes 4194304 | tf_op jit(solution)/shard_map/all_to_all | solution.py:83
  196.8 1.1 reduce_sum.62
  (13 shorter events, 0.1 us)
Async XLA Ops:
  6.5 60.6 %copy-start = (bf16[1024,48]{0,1:T(8,128)(2,1)S(1)}, bf16[1024,48]{0,1:T(8,128)(2,1)}, u32[]{:S(2)}) copy-start(bf16[1024,48]{0,1:T(8,128)(2,1)} %param.9) | copy-start | bytes 294916
  6.5 1.5 copy-start.2
  6.5 1.8 copy-start.1
  6.5 63.4 %all-gather.5.cloned.1.call-start = ((), (), s32[]{:S(2)}) async-start(), calls=%async_computation.2 | async-start | bytes 10485760 | tf_op jit(solution)/shard_map/all_gather | solution.py:63
  7.3 122.5 %all-gather.7.cloned.1.call-start = ((), (), s32[]{:S(2)}) async-start(), calls=%async_computation.3 | async-start | bytes 10485760 | tf_op jit(solution)/shard_map/all_gather | solution.py:69
  8.3 9.1 %copy-start.3 = (s32[8]{0:T(128)S(1)}, s32[8]{0:T(128)}, u32[]{:S(2)}) copy-start(s32[8]{0:T(128)} %param.7) | copy-start | bytes 100
  9.9 55.5 %all-to-all-start = ((bf16[8,128,1024]{2,1,0:T(8,128)(2,1)}), bf16[8,128,1024]{2,1,0:T(8,128)(2,1)S(1)}, u32[]{:S(2)}, u32[]{:S(2)}) async-start(bf16[8,128,1024]{2,1,0:T(8,128)(2,1)} %broadcast_multiply_fusion), calls=%async_computation | async-start | bytes 4194304 | tf_op jit(solution)/shard_map/all_to_all | solution.py:36
  129.8 6.1 %copy-start.4 = (bf16[1,4096,1024]{2,1,0:T(8,128)(2,1)S(1)}, bf16[1,4096,1024]{2,1,0:T(8,128)(2,1)}, u32[]{:S(2)}) copy-start(bf16[1,4096,1024]{2,1,0:T(8,128)(2,1)} %all-gather.7.cloned.1.call-done) | copy-start | bytes 25165828
Sparse Core Ops, SparseCore 0:
  8.9 60.9 all-gather.4
  71.5 58.2 all-gather.6
where the time goes:
time: 205 us
  waiting for transfers between devices  102 us (50%)
  blocking collectives  53.9 us (26%)
  matrix products  22.8 us (11%)
  between operations  13.5 us (7%)
  starting transfers between devices  7.35 us (4%)
  other arithmetic  3.72 us (2%)
    all_to_all x1, blocking collectives, shards(): lax.all_to_all(placed, 'expert', split_axis=0, concat_axis=0, tiled=True)  53.9 us
    all_gather x1, waiting for transfers between devices, shards(): segment = lax.all_gather(w_out[0], 'dp', axis=0, tiled=True)  50.3 us
    all_to_all x1, waiting for transfers between devices, shards(): lax.all_to_all(outgoing, 'expert', split_axis=0, concat_axis=0, tiled=True)  47.8 us
    dot_general x4, matrix products, shards(): jnp.dot(hidden_part, weight_part, preferred_element_type=jnp.float32)  10.3 us
    dot_general x1, matrix products, shards(): jnp.dot(picked, lax.all_gather(w_in[0], 'dp', axis=1, tiled=True), prefer...  9.61 us
    all_to_all x1, starting transfers between devices, shards(): lax.all_to_all(outgoing, 'expert', split_axis=0, concat_axis=0, tiled=True)  7.31 us
  transfers between devices with their start and end apart: 3, of which 3 were waited for; matrix products, arithmetic and copies ran while one was open for 7% of the time, Pallas kernels for 0%

commit v1 on v0

v1 whole, which is shorter than its diff:
```python
import jax
import jax.numpy as jnp
from jax import lax
from jax.sharding import PartitionSpec as P

BLK = 128


def shards(tokens, task_ids, routing, gate_weight, w_in, w_out):
    n_experts = lax.axis_size("expert")
    n_dp = lax.axis_size("dp")
    my_expert = lax.axis_index("expert")
    local_rows, width_model = tokens.shape
    block_total = routing.shape[0]
    block_here = local_rows // BLK
    capacity = 2 * block_here + 1
    chosen = routing == my_expert
    taken_flag = jnp.any(chosen, axis=1).astype(jnp.int32)
    ranked = jnp.cumsum(taken_flag) - taken_flag
    slot_ids = jnp.arange(capacity, dtype=jnp.int32)
    select_mask = (taken_flag[None, :] == 1) & (ranked[None, :] == slot_ids[:, None])
    select_float = select_mask.astype(jnp.bfloat16)
    select_int = select_mask.astype(jnp.int32)
    other_id = jnp.where(chosen[:, 0], routing[:, 1], routing[:, 0])
    slot_task = jnp.sum(select_int * task_ids[None, :], axis=1)
    slot_other = jnp.sum(select_int * other_id[None, :], axis=1)
    slot_valid = jnp.sum(select_int, axis=1).astype(jnp.float32)
    slot_block = jnp.sum(
        select_int * jnp.arange(block_total, dtype=jnp.int32)[None, :], axis=1
    )
    row_tokens = lax.all_gather(tokens, "expert", axis=0, tiled=True)
    picked = jnp.concatenate(
        [
            lax.dynamic_slice_in_dim(row_tokens, slot_block[slot] * BLK, BLK, 0)
            for slot in range(capacity)
        ],
        axis=0,
    )
    column_slots = lax.all_gather(picked, "dp", axis=0, tiled=True)
    hidden = jax.nn.gelu(
        jnp.dot(column_slots, w_in[0], preferred_element_type=jnp.float32)
    ).astype(jnp.bfloat16)
    partial = jnp.dot(hidden, w_out[0], preferred_element_type=jnp.float32).astype(jnp.bfloat16)
    running = lax.psum_scatter(partial, "dp", scatter_dimension=0, tiled=True)

    gate_columns = gate_weight.shape[1]
    logits = jnp.dot(picked, gate_weight, preferred_element_type=jnp.float32).reshape(
        capacity, BLK, gate_columns
    )
    column_ids = jnp.arange(gate_columns, dtype=jnp.int32)
    sign = (column_ids[None, :] == (slot_task * n_experts + my_expert)[:, None]).astype(
        jnp.float32
    ) - (column_ids[None, :] == (slot_task * n_experts + slot_other)[:, None]).astype(jnp.float32)
    weights = (
        jax.nn.sigmoid(jnp.sum(logits * sign[:, None, :], axis=2)) * slot_valid[:, None]
    ).reshape(capacity * BLK)
    gated = (weights[:, None] * running.astype(jnp.float32)).astype(jnp.bfloat16)
    gated = gated.reshape(capacity, BLK, width_model)
    placed = jnp.zeros((block_total, BLK, width_model), jnp.bfloat16)
    for slot in range(capacity):
        placed = jnp.where(select_mask[slot][:, None, None], gated[slot][None], placed)
    return lax.psum_scatter(
        placed.reshape(block_total * BLK, width_model), "expert", scatter_dimension=0, tiled=True
    )


def solution(mesh):
    placed = (
        P(("dp", "expert"), None),
        P("dp"),
        P("dp", None),
        P(),
        P("expert", None, "dp"),
        P("expert", "dp", None),
    )
    return jax.shard_map(
        shards, mesh=mesh, in_specs=placed, out_specs=P(("dp", "expert"), None), check_vma=False
    )
```

time: 205 us -> 218 us (1.063)
  waiting for transfers between devices: 102 us -> 183 us
  blocking collectives: 53.9 us -> 0 us
  matrix products: 22.8 us -> 10.6 us
  starting transfers between devices: 7.35 us -> 0.12 us
  other arithmetic: 3.72 us -> 6.97 us
    reduce_scatter x0 -> x2, waiting for transfers between devices: none -> 106 us  [the longest x1 68.9 us: shards(): lax.psum_scatter(placed.reshape(block_total * BLK, width_model), 'expert'...]
    all_to_all x1 -> x0, blocking collectives: 53.9 us -> none  [shards(): lax.all_to_all(placed, 'expert', split_axis=0, concat_axis=0, tiled=True)]
    all_to_all x1 -> x0, waiting for transfers between devices: 47.8 us -> none  [shards(): lax.all_to_all(outgoing, 'expert', split_axis=0, concat_axis=0, tiled=True)]
    all_gather x2, waiting for transfers between devices: 52.6 us -> 76.2 us  [the longest x1 49 us: shards(): row_tokens = lax.all_gather(tokens, 'expert', axis=0, tiled=True)]
    dot_general x7 -> x1, matrix products: 22.5 us -> 10.2 us  [shards(): jnp.dot(hidden, w_out[0], preferred_element_type=jnp.float32)]
    all_to_all x1 -> x0, starting transfers between devices: 7.31 us -> none  [shards(): lax.all_to_all(outgoing, 'expert', split_axis=0, concat_axis=0, tiled=True)]
  transfers between devices with their start and end apart: 3 -> 4, of which waited for: 3 -> 4; matrix products, arithmetic and copies ran while one was open for 7% -> 2% of each run, Pallas kernels for 0% -> 0%
where the time goes in v1:
time: 218 us
  waiting for transfers between devices  183 us (84%)
  between operations  15.1 us (7%)
  matrix products  10.6 us (5%)
  other arithmetic  6.97 us (3%)
  local copies, waits for them, and re-layouts  2.53 us (1%)
    reduce_scatter x1, waiting for transfers between devices, shards(): lax.psum_scatter(placed.reshape(block_total * BLK, width_model), 'expert'...  68.9 us
    all_gather x1, waiting for transfers between devices, shards(): row_tokens = lax.all_gather(tokens, 'expert', axis=0, tiled=True)  49 us
    reduce_scatter x1, waiting for transfers between devices, shards(): running = lax.psum_scatter(partial, 'dp', scatter_dimension=0, tiled=True)  36.8 us
    all_gather x1, waiting for transfers between devices, shards(): column_slots = lax.all_gather(picked, 'dp', axis=0, tiled=True)  27.1 us
    dot_general x1, matrix products, shards(): jnp.dot(hidden, w_out[0], preferred_element_type=jnp.float32)  10.2 us
  transfers between devices with their start and end apart: 4, of which 4 were waited for; matrix products, arithmetic and copies ran while one was open for 2% of the time, Pallas kernels for 0%

profile of v1, /device:TPU:0, one launch (start us, length us, event | category | flops | bytes accessed | tf_op | source)
XLA Modules:
  0.0 217.9 jit_solution(16350522476642334610)
XLA Ops:
  6.5 0.0 copy-start
  6.5 0.7 all-gather.3.cloned.1.call-update
  7.3 0.0 all-gather.5.cloned.1.call-start
  7.3 0.7 fusion.30
  8.0 0.2 reduce-window.8
  8.2 0.8 fusion.24
  9.0 0.8 convert_reduce_fusion
  9.8 0.6 fusion.32
  12.3 49.0 %all-gather.3.cloned.1.call-done = bf16[1024,1024]{1,0:T(8,128)(2,1)} async-done(((bf16[128,1024]{1,0:T(8,128)(2,1)}), bf16[1024,1024]{1,0:T(8,128)(2,1)}) %all-gather.3.cloned.1.call-update) | async-done | bytes 2097168 | tf_op jit(solution)/shard_map/all_gather | solution.py:31
  61.3 1.2 constant_dynamic-slice_fusion.2
  62.5 0.9 pad_maximum_fusion
  63.4 0.0 all-gather.5.cloned.1.call-update
  63.4 0.0 reduce-scatter.3.cloned.1.call-start
  63.5 27.1 %all-gather.5.cloned.1.call-done = bf16[1536,1024]{1,0:T(8,128)(2,1)} async-done(((bf16[384,1024]{1,0:T(8,128)(2,1)}), bf16[1536,1024]{1,0:T(8,128)(2,1)}) %all-gather.5.cloned.1.call-update) | async-done | bytes 3145744 | tf_op jit(solution)/shard_map/all_gather | solution.py:39
  90.6 0.0 copy-done
  90.6 10.2 %convolution_convert_fusion = bf16[1536,1024]{1,0:T(8,128)(2,1)} fusion(bf16[1,1024,1024]{2,1,0:T(8,128)(2,1)S(1)} %copy-done, bf16[1536,1024]{1,0:T(8,128)(2,1)} %all-gather.5.cloned.1.call-done, bf16[1,1024,1024]{2,1,0:T(8,128)(2,1)} %param.10), kind=kOutput, calls=%fused_computation.9 | convolution fusion | flops 6458179584 | bytes 10485760 | tf_op jit(solution)/shard_map/dot_general | solution.py:43
  100.8 0.0 reduce-scatter.3.cloned.1.call-update
  100.9 0.0 reduce-scatter.5.cloned.1.call-start
  100.9 0.1 convert_subtract_fusion
  101.0 0.1 copy.7
  101.1 0.1 broadcast_bitcast_fusion.2
  101.2 0.1 broadcast_bitcast_fusion
  101.3 0.1 mul.120
  101.4 0.4 copy-done.1
  101.7 0.4 fusion.22
  102.1 0.1 divide_multiply_fusion
  102.2 36.8 %reduce-scatter.3.cloned.1.call-done = bf16[384,1024]{1,0:T(8,128)(2,1)} async-done(((bf16[1536,1024]{1,0:T(8,128)(2,1)}), bf16[384,1024]{1,0:T(8,128)(2,1)}) %reduce-scatter.3.cloned.1.call-update) | async-done | bytes 786448 | tf_op jit(solution)/shard_map/reduce_scatter | solution.py:44
  139.0 1.3 multiply_convert_fusion
  140.3 0.1 fusion.31
  140.4 2.1 fusion.14
  142.5 0.0 reduce-scatter.5.cloned.1.call-update
  142.5 68.9 %reduce-scatter.5.cloned.1.call-done = bf16[128,1024]{1,0:T(8,128)(2,1)} async-done(((bf16[1024,1024]{1,0:T(8,128)(2,1)}), bf16[128,1024]{1,0:T(8,128)(2,1)}) %reduce-scatter.5.cloned.1.call-update) | async-done | bytes 262160 | tf_op jit(solution)/shard_map/reduce_scatter | solution.py:62
  (7 shorter events, 0.0 us)
Async XLA Ops:
  6.5 84.1 %copy-start = (bf16[1,1024,1024]{2,1,0:T(8,128)(2,1)S(1)}, bf16[1,1024,1024]{2,1,0:T(8,128)(2,1)}, u32[]{:S(2)}) copy-start(bf16[1,1024,1024]{2,1,0:T(8,128)(2,1)} %param.11) | copy-start | bytes 6291460
  6.5 54.8 %all-gather.3.cloned.1.call-start = ((), (), s32[]{:S(2)}) async-start(), calls=%async_computation.2 | async-start | bytes 2359296 | tf_op jit(solution)/shard_map/all_gather | solution.py:31
  7.3 83.4 %all-gather.5.cloned.1.call-start = ((), (), s32[]{:S(2)}) async-start(), calls=%async_computation.3 | async-start | bytes 3932160 | tf_op jit(solution)/shard_map/all_gather | solution.py:39
  63.4 75.5 %reduce-scatter.3.cloned.1.call-start = ((), (), s32[]{:S(2)}) async-start(), calls=%async_computation.4 | async-start | bytes 3932160 | tf_op jit(solution)/shard_map/reduce_scatter | solution.py:44
  100.8 0.9 copy-start.1
  100.9 110.5 %reduce-scatter.5.cloned.1.call-start = ((), (), s32[]{:S(2)}) async-start(), calls=%async_computation.5 | async-start | bytes 2359296 | tf_op jit(solution)/shard_map/reduce_scatter | solution.py:62
Sparse Core Ops, SparseCore 0:
  9.5 51.8 all-gather.2
  63.6 27.0 all-gather.4
  101.0 37.9 reduce-scatter.2
  142.6 68.6 reduce-scatter.4

commit v2 on v1

v2 whole, which is shorter than its diff:
```python
import functools

import jax
import jax.numpy as jnp
from jax import lax
from jax.experimental import pallas as pl
from jax.experimental.pallas import tpu as pltpu
from jax.sharding import PartitionSpec as P

BLK = 128
PARTS = 2
SKEW = 9.0
TILE = 256
MESH = pl.DeviceIdType.MESH


def gelu(x):
    return 0.5 * x * (1.0 + jnp.tanh(0.7978845608028654 * (x + 0.044715 * (x * x * x))))


def kernel(
    n, n_dp, capacity,
    routing, tasks, tokens, gate_weight, w_in_hbm, w_out_hbm, out,
    w_in, w_out, rings, cols, hidden, acc, pout, pin, xs, xr, gated, weights, rs_out, rs_in,
    w_sem, ag_s, ag_r, x_s, x_r, b_s, b_r, p_s, p_r, y_s, y_r, r_s, r_r,
):
    d_model = tokens.shape[1]
    chips = n_dp // 2
    half_ring = n // 2
    rows = BLK // PARTS
    mid = rows // 2
    wide = capacity * rows
    me = lax.axis_index("expert")
    my_dp = lax.axis_index("dp")
    my_x, my_core = my_dp // 2, my_dp % 2

    def pos_of(e):
        c, k = e % 2, e // 2
        return (1 - c) * k + c * (n - 1 - k)

    def expert_at(p):
        h = p // half_ring
        return (1 - h) * (2 * p) + h * (2 * (n - 1 - p) + 1)

    my_pos = pos_of(me)
    right = {"expert": expert_at((my_pos + 1) % n)}
    left = {"expert": expert_at((my_pos + n - 1) % n)}
    sibling = {"dp": my_x * 2 + 1 - my_core}

    def chip(k):
        return {"dp": ((my_x + k) % chips) * 2 + my_core}

    load_in = pltpu.make_async_copy(w_in_hbm.at[0], w_in, w_sem.at[0])
    load_out = pltpu.make_async_copy(w_out_hbm.at[0], w_out, w_sem.at[1])
    load_in.start()
    load_out.start()

    barrier = pltpu.get_barrier_semaphore()
    partners = [left, right, sibling] + [chip(k) for k in range(1, chips)]
    for partner in partners:
        pl.semaphore_signal(barrier, inc=1, device_id=partner, device_id_type=MESH)
    pl.semaphore_wait(barrier, len(partners))

    def remote(src, dst, send, recv, target):
        return pltpu.make_async_remote_copy(
            src_ref=src, dst_ref=dst, send_sem=send, recv_sem=recv,
            device_id=target, device_id_type=MESH,
        )

    sent = []

    def go(copy):
        copy.start()
        sent.append(copy)

    def span(s, way, last):
        if s != last:
            return pl.ds(0, rows)
        return pl.ds(0, mid) if way == 0 else pl.ds(mid, rows - mid)

    def ag_copy(h, way, s):
        source = (-s) % n if way == 0 else s % n
        target = (-s - 1) % n if way == 0 else (s + 1) % n
        part = span(s, way, half_ring - 1)
        if s == 0:
            begin = h * rows + (mid if way == 1 and half_ring == 1 else 0)
            src = tokens.at[pl.ds(begin, part.size)]
        else:
            src = rings[h].at[source, part]
        return remote(
            src, rings[h].at[target, part], ag_s.at[h, way, s], ag_r.at[h, way, s],
            right if way == 0 else left,
        )

    def ag_stage(h, s):
        for way in range(2):
            if s > 0:
                ag_copy(h, way, s - 1).wait_recv()
            go(ag_copy(h, way, s))

    taken, rank, count = [], [], 0
    for m in range(n):
        first, second = routing[m, 0], routing[m, 1]
        hit = jnp.where(first == me, 1, 0) + jnp.where(second == me, 1, 0)
        taken.append(hit)
        rank.append(count)
        count = count + hit
    slot_block, slot_other, slot_task, slot_valid = [], [], [], []
    for slot in range(capacity):
        at, other, task, valid = 0, 0, 0, 0
        for m in range(n):
            here = taken[m] * jnp.where(rank[m] == slot, 1, 0)
            at = at + here * ((pos_of(m) + n - my_pos) % n)
            other = other + here * (routing[m, 0] + routing[m, 1] - me)
            task = task + here * tasks[m]
            valid = valid + here
        slot_block.append(jnp.clip(at, 0, n - 1))
        slot_other.append(other)
        slot_task.append(task)
        slot_valid.append(valid)

    def slot_of(offset):
        e = expert_at((my_pos + offset + 2 * n) % n)
        hit = jnp.where(routing[e, 0] == me, 1, 0) + jnp.where(routing[e, 1] == me, 1, 0)
        before = 0
        for m in range(n):
            before = before + taken[m] * jnp.where(m < e, 1, 0)
        return jnp.clip(hit * before + (1 - hit) * capacity, 0, capacity)

    slots_at = [slot_of(k) for k in range(n)]

    def x_copy(h, k):
        return remote(
            cols.at[h, 0, 0], cols.at[h, chips - k, 0], x_s.at[h, k], x_r.at[h, chips - k], chip(k)
        )

    def b_copy(h, k):
        return remote(cols.at[h, k, 0], cols.at[h, k, 1], b_s.at[h, k], b_r.at[h, k], sibling)

    def select_stage(h):
        for way in range(2):
            ag_copy(h, way, half_ring - 1).wait_recv()
        rings[h][0] = tokens[h * rows : (h + 1) * rows, :]
        for slot in range(capacity):
            cols[h, 0, 0, slot * rows : (slot + 1) * rows, :] = rings[h][slot_block[slot]]
        mine = cols[h, 0, 0]
        logits = jnp.dot(mine, gate_weight[...], preferred_element_type=jnp.float32)
        column = lax.broadcasted_iota(jnp.int32, (rows, logits.shape[1]), 1)
        for slot in range(capacity):
            own = slot_task[slot] * n + me
            against = slot_task[slot] * n + slot_other[slot]
            sign = jnp.where(column == own, 1.0, 0.0) - jnp.where(column == against, 1.0, 0.0)
            gap = jnp.sum(
                logits[slot * rows : (slot + 1) * rows] * sign, axis=1, keepdims=True
            )
            gate = jax.nn.sigmoid(gap) * slot_valid[slot].astype(jnp.float32)
            weights[h, slot * rows : (slot + 1) * rows, :] = jnp.broadcast_to(gate, (rows, 128))
        for k in range(1, chips):
            go(x_copy(h, k))
        go(b_copy(h, 0))

    def x_recv(h, k):
        return remote(
            cols.at[h, 0, 0], cols.at[h, k, 0], x_s.at[h, chips - k], x_r.at[h, k], chip(chips - k)
        )

    def p_copy(h, k):
        return remote(pout.at[h, k], pin.at[h, k], p_s.at[h, k], p_r.at[h, k], sibling)

    def y_copy(h, k):
        return remote(
            xs.at[h, k], xr.at[h, chips - k], y_s.at[h, k], y_r.at[h, chips - k], chip(k)
        )

    def y_recv(h, k):
        return remote(
            xs.at[h, chips - k], xr.at[h, k], y_s.at[h, chips - k], y_r.at[h, k], chip(chips - k)
        )

    def forward_stage(h, k):
        x_recv(h, k).wait_recv()
        go(b_copy(h, k))

    def expert_stage(h, k):
        b_copy(h, k).wait_recv()
        lhs = cols.at[h, k]

        @pl.loop(0, w_in.shape[1] // TILE)
        def _(t):
            at = pl.ds(pl.multiple_of(t * TILE, TILE), TILE)
            x = lhs[...].reshape(2 * wide, d_model)
            y = jnp.dot(x, w_in[:, at], preferred_element_type=jnp.float32)
            hidden[:, at] = gelu(y).astype(jnp.bfloat16)

        @pl.loop(0, d_model // TILE)
        def _(t):
            at = pl.ds(pl.multiple_of(t * TILE, TILE), TILE)
            y = jnp.dot(hidden[...], w_out[:, at], preferred_element_type=jnp.float32)
            acc[h, k, :, at] = y[:wide]
            pout[h, k, :, at] = y[wide:].astype(jnp.bfloat16)

        go(p_copy(h, k))

    def return_stage(h, k):
        p_copy(h, k).wait_recv()
        xs[h, k] = (acc[h, k] + pin[h, k].astype(jnp.float32)).astype(jnp.bfloat16)
        go(y_copy(h, k))

    def gate_stage(h):
        p_copy(h, 0).wait_recv()
        for k in range(1, chips):
            y_recv(h, k).wait_recv()
        for slot in range(capacity):
            at = slice(slot * rows, (slot + 1) * rows)
            total = acc[h, 0, at, :] + pin[h, 0, at, :].astype(jnp.float32)
            for k in range(1, chips):
                total = total + xr[h, k, at, :].astype(jnp.float32)
            gated[h, slot] = (weights[h, at, :1] * total).astype(jnp.bfloat16)
        gated[h, capacity] = jnp.zeros((rows, d_model), jnp.bfloat16)

    def rs_copy(h, way, s):
        part = span(s, way, 0)
        return remote(
            rs_out.at[h, way, s, part], rs_in.at[h, way, s, part],
            r_s.at[h, way, s], r_r.at[h, way, s], right if way == 0 else left,
        )

    def share(h, offset):
        return gated[h, slots_at[offset % n]]

    def add(a, b):
        return (a.astype(jnp.float32) + b.astype(jnp.float32)).astype(jnp.bfloat16)

    def half(way):
        return slice(0, mid) if way == 0 else slice(mid, rows)

    def rs_stage(h, s):
        for way in range(2):
            offset = half_ring - s if way == 0 else s - half_ring
            rs_out[h, way, s] = share(h, offset)
            if s > 0:
                rs_copy(h, way, s - 1).wait_recv()
                at = half(way) if s == 1 else slice(0, rows)
                rs_out[h, way, s, at, :] = add(rs_out[h, way, s, at, :], rs_in[h, way, s - 1, at, :])
            go(rs_copy(h, way, s))

    def out_stage(h):
        for way in range(2):
            rs_copy(h, way, half_ring - 1).wait_recv()
        total = share(h, 0).astype(jnp.float32)
        for way in range(2):
            if half_ring > 1:
                total = total + rs_in[h, way, half_ring - 1].astype(jnp.float32)
        out[h * rows : (h + 1) * rows, :] = total.astype(jnp.bfloat16)

    def loaded(h):
        if h == 0:
            load_in.wait()
            load_out.wait()

    stages = []
    for h in range(PARTS):
        clock = h * SKEW

        def plan(when, *call):
            stages.append((when, len(stages), functools.partial(*call)))

        for s in range(half_ring):
            plan(h * 0.6 * SKEW + 4.0 * s, ag_stage, h, s)
        base = h * SKEW + 4.0 * half_ring
        plan(base, select_stage, h)
        plan(base + 1.0, loaded, h)
        plan(base + 1.1, expert_stage, h, 0)
        for k in range(1, chips):
            plan(base + 10.0 + k, forward_stage, h, k)
            plan(base + 12.0 + k, expert_stage, h, k)
            plan(base + 14.0 + k, return_stage, h, k)
        base = base + 24.0 + chips
        plan(base, gate_stage, h)
        for s in range(half_ring):
            plan(base + 0.5 + 4.0 * s, rs_stage, h, s)
        plan(base + 0.5 + 4.0 * half_ring, out_stage, h)
    for _, _, stage in sorted(stages, key=lambda item: item[:2]):
        stage()
    for copy in sent:
        copy.wait_send()


def shards(tokens, task_ids, routing, gate_weight, w_in, w_out):
    n = lax.axis_size("expert")
    n_dp = lax.axis_size("dp")
    d_model = tokens.shape[1]
    capacity = 2 * (tokens.shape[0] // BLK) + 1
    chips, half_ring = n_dp // 2, n // 2
    rows = BLK // PARTS
    wide = capacity * rows
    bf16 = jnp.bfloat16
    dma = pltpu.SemaphoreType.DMA
    vmem = pl.BlockSpec(memory_space=pltpu.VMEM)
    smem = pl.BlockSpec(memory_space=pltpu.SMEM)
    hbm = pl.BlockSpec(memory_space=pl.ANY)
    return pl.pallas_call(
        functools.partial(kernel, n, n_dp, capacity),
        out_shape=jax.ShapeDtypeStruct(tokens.shape, bf16),
        in_specs=[smem, smem, vmem, vmem, hbm, hbm],
        out_specs=vmem,
        scratch_shapes=[
            pltpu.VMEM(w_in.shape[1:], bf16),
            pltpu.VMEM(w_out.shape[1:], bf16),
            [pltpu.VMEM((n, rows, d_model), bf16) for _ in range(PARTS)],
            pltpu.VMEM((PARTS, chips, 2, wide, d_model), bf16),
            pltpu.VMEM((2 * wide, w_in.shape[2]), bf16),
            pltpu.VMEM((PARTS, chips, wide, d_model), jnp.float32),
            pltpu.VMEM((PARTS, chips, wide, d_model), bf16),
            pltpu.VMEM((PARTS, chips, wide, d_model), bf16),
            pltpu.VMEM((PARTS, chips, wide, d_model), bf16),
            pltpu.VMEM((PARTS, chips, wide, d_model), bf16),
            pltpu.VMEM((PARTS, capacity + 1, rows, d_model), bf16),
            pltpu.VMEM((PARTS, wide, 128), jnp.float32),
            pltpu.VMEM((PARTS, 2, half_ring, rows, d_model), bf16),
            pltpu.VMEM((PARTS, 2, half_ring, rows, d_model), bf16),
            dma((2,)),
            dma((PARTS, 2, half_ring)),
            dma((PARTS, 2, half_ring)),
            dma((PARTS, chips)),
            dma((PARTS, chips)),
            dma((PARTS, chips)),
            dma((PARTS, chips)),
            dma((PARTS, chips)),
            dma((PARTS, chips)),
            dma((PARTS, chips)),
            dma((PARTS, chips)),
            dma((PARTS, 2, half_ring)),
            dma((PARTS, 2, half_ring)),
        ],
        compiler_params=pltpu.CompilerParams(
            collective_id=0, has_side_effects=True, vmem_limit_bytes=64 * 1024 * 1024 - 65536
        ),
    )(routing, task_ids, tokens, gate_weight, w_in, w_out)


def solution(mesh):
    placed = (
        P(("dp", "expert"), None),
        P("dp"),
        P("dp", None),
        P(),
        P("expert", None, "dp"),
        P("expert", "dp", None),
    )
    return jax.shard_map(
        shards, mesh=mesh, in_specs=placed, out_specs=P(("dp", "expert"), None), check_vma=False
    )
```

time: 218 us -> 91.7 us (0.42)
  waiting for transfers between devices: 183 us -> 0 us
  Pallas kernels: 0 us -> 86.8 us
  between operations: 15.1 us -> 0.01 us
  matrix products: 10.6 us -> 0 us
  other arithmetic: 6.97 us -> 0 us
  local copies, waits for them, and re-layouts: 2.53 us -> 4.74 us
    reduce_scatter x2 -> x0, waiting for transfers between devices: 106 us -> none  [the longest x1 68.9 us: shards(): lax.psum_scatter(placed.reshape(block_total * BLK, width_model), 'expert'...]
    pallas_call x0 -> x1, Pallas kernels: none -> 86.8 us  [shards(): pl.pallas_call(functools.partial(kernel, n, n_dp, capacity), out_shape=ja...]
    all_gather x2 -> x0, waiting for transfers between devices: 76.2 us -> none  [the longest x1 49 us: shards(): row_tokens = lax.all_gather(tokens, 'expert', axis=0, tiled=True)]
    dot_general x2 -> x0, matrix products: 10.6 us -> none  [the longest x1 10.2 us: shards(): jnp.dot(hidden, w_out[0], preferred_element_type=jnp.float32)]
    unnamed x4 -> x3, local copies, waits for them, and re-layouts: 0.36 us -> 4.74 us
    select_n x2 -> x0, other arithmetic: 2.86 us -> none  [the longest x1 2.11 us: shards(): jnp.where(select_mask[slot][:, None, None], gated[slot][None], placed)]
  transfers between devices with their start and end apart: 4 -> 0, of which waited for: 4 -> 0; matrix products, arithmetic and copies ran while one was open for 2% -> 0% of each run, Pallas kernels for 0% -> 0%
where the time goes in v2:
time: 91.7 us; the launch traced here: 91.5 us
  Pallas kernels  86.8 us (95%)
  local copies, waits for them, and re-layouts  4.74 us (5%)
    pallas_call x1, Pallas kernels, shards(): pl.pallas_call(functools.partial(kernel, n, n_dp, capacity), out_shape=ja...  86.8 us
    unnamed x3, local copies, waits for them, and re-layouts  4.74 us

profile of v2, /device:TPU:0, one launch (start us, length us, event | category | flops | bytes accessed | tf_op | source)
XLA Modules:
  0.0 91.5 jit_solution(12339818224755192135)
XLA Ops:
  0.0 1.3 %copy.7.routing = s32[8,2]{1,0:T(8,128)} copy(s32[8,2]{0,1:T(2,128)} %param.8) | data formatting | bytes 128 | tf_op args[2]
  1.3 1.7 %copy.8.gate_weight = bf16[1024,48]{1,0:T(8,128)(2,1)} copy(bf16[1024,48]{0,1:T(8,128)(2,1)} %param.9) | data formatting | bytes 196608 | tf_op args[3]
  3.1 86.8 %shard_map.64 = bf16[128,1024]{1,0:T(8,128)(2,1)} custom-call(s32[8,2]{1,0:T(8,128)} %copy.7.routing, s32[8]{0:T(128)} %tasks.1, bf16[128,1024]{1,0:T(8,128)(2,1)} %tokens.1, bf16[1024,48]{1,0:T(8,128)(2,1)} %copy.8.gate_weight, bf16[1,1024,1024]{2,1,0:T(8,128)(2,1)} %w_in_hbm.1, bf16[1,1024,1024]{2,1,0:T(8,128)(2,1)} %w_out_hbm.1), custom_call_target="tpu_custom_call" | custom-call | tf_op jit(solution)/shard_map/pallas_call | solution.py:302
  89.8 1.7 %copy.10 = bf16[128,1024]{1,0:T(8,128)(2,1)} copy(bf16[128,1024]{1,0:T(8,128)(2,1)} %shard_map.64) | data formatting | bytes 524288

commit v3 on v2

--- a/solution.py
+++ b/solution.py
@@ -9,7 +9,7 @@
 
 BLK = 128
 PARTS = 2
-SKEW = 9.0
+SKEW = 2.0
 TILE = 256
 MESH = pl.DeviceIdType.MESH
 
@@ -97,6 +97,9 @@
             if s > 0:
                 ag_copy(h, way, s - 1).wait_recv()
             go(ag_copy(h, way, s))
+
+    for h in range(PARTS):
+        ag_stage(h, 0)
 
     taken, rank, count = [], [], 0
     for m in range(n):
@@ -260,12 +263,11 @@
 
     stages = []
     for h in range(PARTS):
-        clock = h * SKEW
 
         def plan(when, *call):
             stages.append((when, len(stages), functools.partial(*call)))
 
-        for s in range(half_ring):
+        for s in range(1, half_ring):
             plan(h * 0.6 * SKEW + 4.0 * s, ag_stage, h, s)
         base = h * SKEW + 4.0 * half_ring
         plan(base, select_stage, h)

time: 91.7 us -> 87.6 us (0.955)
  Pallas kernels: 86.8 us -> 82.7 us
    pallas_call x1, Pallas kernels: 86.8 us -> 82.7 us  [shards(): pl.pallas_call(functools.partial(kernel, n, n_dp, capacity), out_shape=ja...]
where the time goes in v3:
time: 87.6 us; the launch traced here: 87.4 us
  Pallas kernels  82.7 us (94%)
  local copies, waits for them, and re-layouts  4.74 us (5%)
    pallas_call x1, Pallas kernels, shards(): pl.pallas_call(functools.partial(kernel, n, n_dp, capacity), out_shape=ja...  82.7 us
    unnamed x3, local copies, waits for them, and re-layouts  4.74 us

profile of v3, /device:TPU:0, one launch (start us, length us, event | category | flops | bytes accessed | tf_op | source)
XLA Modules:
  0.0 87.4 jit_solution(8353351781135445402)
XLA Ops:
  0.0 1.3 %copy.7.routing = s32[8,2]{1,0:T(8,128)} copy(s32[8,2]{0,1:T(2,128)} %param.8) | data formatting | bytes 128 | tf_op args[2]
  1.3 1.7 %copy.8.gate_weight = bf16[1024,48]{1,0:T(8,128)(2,1)} copy(bf16[1024,48]{0,1:T(8,128)(2,1)} %param.9) | data formatting | bytes 196608 | tf_op args[3]
  3.1 82.7 %shard_map.64 = bf16[128,1024]{1,0:T(8,128)(2,1)} custom-call(s32[8,2]{1,0:T(8,128)} %copy.7.routing, s32[8]{0:T(128)} %tasks.1, bf16[128,1024]{1,0:T(8,128)(2,1)} %tokens.1, bf16[1024,48]{1,0:T(8,128)(2,1)} %copy.8.gate_weight, bf16[1,1024,1024]{2,1,0:T(8,128)(2,1)} %w_in_hbm.1, bf16[1,1024,1024]{2,1,0:T(8,128)(2,1)} %w_out_hbm.1), custom_call_target="tpu_custom_call" | custom-call | tf_op jit(solution)/shard_map/pallas_call | solution.py:304
  85.7 1.7 %copy.10 = bf16[128,1024]{1,0:T(8,128)(2,1)} copy(bf16[128,1024]{1,0:T(8,128)(2,1)} %shard_map.64) | data formatting | bytes 524288
